TPU v7x, 128 devices: a whole 4x4x4 slice. The times are simulated.
128 devices in a mesh: dim: 16 (over y, x), batch: 8 (over z, core).
Axes of the slice: x: 4, y: 4, z: 4, core: 2. Of those that a mesh axis runs over, the one named last changes fastest.
Arguments:
- start: float32 [2048, 4096], P('batch', 'dim'), may hold values from -6 to 6
- increments: float32 [3, 2048, 4096], P(None, 'batch', 'dim'), may hold values from -0.75 to 0.75
- w_in: bfloat16 [4096, 4096], P(None, 'dim'), may hold values from -0.09375 to 0.09375
- w_out: bfloat16 [4096, 4096], P('dim'), may hold values from -0.09375 to 0.09375
- initial: float32 [], replicated, may hold values from 4 to 5.5
Outputs:
- residual: float32 [2048], P('batch')
- grad_in: float32 [4096, 4096], P('batch', 'dim')
- grad_out: float32 [4096, 4096], P('dim', 'batch')
All inputs are finite; a program needn't handle non-finite values.
Results may differ from a plain program's by a relative error of at most 0.0051.
Values may be sent and summed in bfloat16 or wider, within the bound.
A program may use at most 128 MiB of HBM per device.

v0:
```python
import math
import jax
import jax.numpy as jnp
from jax import lax
from jax.sharding import Mesh
from jax.sharding import PartitionSpec as P

D = 4096
STEPS = 3
DIM = ("y", "x")
BATCH = ("z", "c")
time_step = 1.0 / 64.0
lam_coef = 50.0
noise_coef = math.sqrt(2.0)


def a2a(array, axis):
    return lax.all_to_all(array, axis, split_axis=0, concat_axis=0, tiled=True)


def scatter_sum(parts, axis):
    got = a2a(parts.astype(jnp.bfloat16), axis)
    return jnp.sum(got.astype(jnp.float32), 0)


def on_device(start, increments, w_in, w_out, initial):
    zscale = 2.0 / math.sqrt(D)
    rows, width = start.shape
    f32, bf16 = (jnp.float32, jnp.bfloat16)
    win = a2a(w_in.reshape(4, 4, width, width).transpose(1, 0, 2, 3), "x")
    wout = a2a(w_out.reshape(width, 4, 4, width).transpose(2, 1, 0, 3), "x")
    states = [start]
    for step in range(STEPS):
        states.append(states[-1] + noise_coef * increments[step])
    xb = jnp.stack(states[:STEPS]).astype(bf16).reshape(STEPS * rows, width)
    inc = increments.reshape(STEPS * rows, width)
    xg = lax.all_gather(xb, "y")
    h = scatter_sum(jnp.einsum("jrd,ijdh->irh", xg, win, preferred_element_type=f32), "x")
    act = jax.nn.silu(h).astype(bf16)
    ag = lax.all_gather(act, "x")
    z = zscale * scatter_sum(jnp.einsum("irh,ijhd->jrd", ag, wout, preferred_element_type=f32), "y")
    terms = jnp.sum(
        (0.5 * lam_coef * time_step * z * z + z * inc).reshape(STEPS, rows, width), (0, 2)
    )
    norm = jnp.sum(states[STEPS] * states[STEPS], 1)
    both = lax.psum(jnp.stack([terms, norm]), DIM)
    residual = initial + both[0] - jnp.log((1.0 + both[1]) * 0.5)
    scale = jnp.tile(zscale * residual, STEPS)[:, None]
    gz = (scale * (lam_coef * time_step * z + inc)).astype(bf16)
    gg = lax.all_gather(gz, "y")
    ga = scatter_sum(jnp.einsum("jrd,ijhd->irh", gg, wout, preferred_element_type=f32), "x")
    sig = jax.nn.sigmoid(h)
    gh = (ga * sig * (1.0 + h * (1.0 - sig))).astype(bf16)
    hg = lax.all_gather(gh, "x")
    gout = jnp.einsum("irh,jrd->jihd", ag, gg, preferred_element_type=f32)
    gin = jnp.einsum("jrd,irh->jidh", xg, hg, preferred_element_type=f32)
    grads = jnp.stack([gin, gout], 1)
    grads = grads.reshape(4, 2, 2, 2, width, width).transpose(3, 0, 1, 2, 4, 5)
    grads = lax.psum_scatter(grads.reshape(2, 4, -1), "c", scatter_dimension=0, tiled=False)
    grads = scatter_sum(grads, "z").reshape(2, 2, width, width)
    grads = lax.all_gather(grads, "c")
    grads = grads.transpose(2, 0, 1, 3, 4).reshape(4, -1)
    grads = a2a(grads.astype(bf16), "x").astype(f32).reshape(2, 2, 2, width, width)
    mine = lax.dynamic_index_in_dim(grads, lax.axis_index("c"), 0, keepdims=False)
    return (
        residual,
        mine[:, 0].reshape(2 * width, width),
        mine[:, 1].transpose(1, 0, 2).reshape(width, 2 * width),
    )


def solution(mesh):
    finer = Mesh(mesh.devices.reshape(4, 4, 4, 2), ("y", "x", "z", "c"))
    return jax.shard_map(
        on_device,
        mesh=finer,
        in_specs=(P(BATCH, DIM), P(None, BATCH, DIM), P(None, DIM), P(DIM, None), P()),
        out_specs=(P(BATCH), P(BATCH, DIM), P(DIM, BATCH)),
        check_vma=False,
    )
```

profile of v0, /device:TPU:1, one launch (start us, length us, event | category | flops | bytes accessed | tf_op | source)
XLA Modules:
  0.0 433.0 jit_solution(6734123639831771158)
XLA Ops:
  7.2 0.0 all-gather.6.cloned.1.call-start
  7.2 1.6 convert_bitcast_fusion.2
  8.8 0.8 pad_maximum_fusion
  9.6 0.0 all-gather.6.cloned.1.call-update
  9.6 0.0 all-gather.8.cloned.1.call-start
  9.7 0.1 copy.66
  9.8 30.1 %all_to_all.37 = bf16[4,4,256,256]{3,2,1,0:T(8,128)(2,1)S(1)} all-to-all(bf16[4,4,256,256]{3,2,1,0:T(8,128)(2,1)S(1)} %bitcast.164), channel_id=1, replica_groups=mesh['y'=4,'x'=4,'z'=4,'c'=2] {'x'}, dimensions={0} | all-to-all | bytes 4194304 | tf_op jit(solution)/shard_map/all_to_all | solution.py:18
  39.9 3.2 fusion.10
  43.1 23.3 %all_to_all.38 = bf16[4,768,256]{2,1,0:T(8,128)(2,1)S(1)} all-to-all(bf16[4,768,256]{2,1,0:T(8,128)(2,1)S(1)} %fusion.10), channel_id=1, replica_groups=mesh['y'=4,'x'=4,'z'=4,'c'=2] {'x'}, dimensions={0} | all-to-all | bytes 3145728 | tf_op jit(solution)/shard_map/all_to_all | solution.py:18
  66.4 0.2 convert_reduce_fusion.3
  66.7 1.0 fusion.26
  67.7 0.5 copy-done.2
  68.2 2.5 copy.43
  70.6 2.8 copy.44
  73.4 40.7 %all_to_all.39 = bf16[4,4,256,256]{3,2,1,0:T(8,128)(2,1)} all-to-all(bf16[4,4,256,256]{3,2,1,0:T(8,128)(2,1)S(1)} %copy.44), channel_id=1, replica_groups=mesh['y'=4,'x'=4,'z'=4,'c'=2] {'x'}, dimensions={0} | all-to-all | bytes 4194304 | tf_op jit(solution)/shard_map/all_to_all | solution.py:18
  114.1 1.5 all-gather.8.cloned.1.call-done
  115.6 5.1 %fusion.16 = bf16[4,768,256]{2,1,0:T(8,128)(2,1)} fusion(bf16[4,4,256,256]{3,2,1,0:T(8,128)(2,1)} %all_to_all.39, bf16[4,768,256]{2,1,0:T(8,128)(2,1)} %all-gather.8.cloned.1.call-done), kind=kOutput, calls=%fused_computation.23 | convolution fusion | flops 1611399168 | bytes 5242880 | tf_op jit(solution)/shard_map/irh,ijhd->jrd/dot_general | solution.py:41
  120.7 4.3 %all-to-all-start.3 = ((bf16[4,768,256]{2,1,0:T(8,128)(2,1)}), bf16[4,768,256]{2,1,0:T(8,128)(2,1)}, u32[]{:S(2)}, u32[]{:S(2)}) async-start(bf16[4,768,256]{2,1,0:T(8,128)(2,1)} %fusion.16), calls=%async_computation.3 | async-start | bytes 3145728 | tf_op jit(solution)/shard_map/all_to_all | solution.py:18
  125.1 0.0 all-gather.10.cloned.1.call-start
  125.8 19.2 %all-to-all-done.3 = bf16[4,768,256]{2,1,0:T(8,128)(2,1)} async-done(((bf16[4,768,256]{2,1,0:T(8,128)(2,1)}), bf16[4,768,256]{2,1,0:T(8,128)(2,1)}, u32[]{:S(2)}, u32[]{:S(2)}) %all-to-all-start.3) | async-done | bytes 1572896 | tf_op jit(solution)/shard_map/all_to_all | solution.py:18
  145.0 1.7 convert_reduce_fusion.2
  146.7 0.1 broadcast_multiply_fusion.1
  146.9 0.2 multiply_reduce_fusion
  147.1 28.5 %psum.7 = f32[2,256]{1,0:T(2,128)S(1)} all-reduce(f32[2,256]{1,0:T(2,128)S(1)} %pad_maximum_fusion.1), channel_id=1, replica_groups=mesh['y'=4,'x'=4,'z'=4,'c'=2] {'y','x'}, use_global_device_ids=true, to_apply=%region_4.5 | all-reduce | flops 512 | bytes 4096 | tf_op jit(solution)/shard_map/psum | solution.py:46
  175.6 0.6 broadcast_multiply_fusion.2
  176.2 0.9 fusion.22
  177.1 0.0 all-gather.12.cloned.1.call-start
  177.2 31.8 %all-gather.10.cloned.1.call-done = bf16[4,768,256]{2,1,0:T(8,128)(2,1)} async-done(((bf16[1,768,256]{2,1,0:T(8,128)(2,1)}), bf16[4,768,256]{2,1,0:T(8,128)(2,1)}) %all-gather.10.cloned.1.call-update) | async-done | bytes 1572880 | tf_op jit(solution)/shard_map/all_gather | solution.py:50
  209.0 3.9 fusion.13
  212.9 23.5 %all_to_all.40 = bf16[4,768,256]{2,1,0:T(8,128)(2,1)S(1)} all-to-all(bf16[4,768,256]{2,1,0:T(8,128)(2,1)S(1)} %fusion.13), channel_id=1, replica_groups=mesh['y'=4,'x'=4,'z'=4,'c'=2] {'x'}, dimensions={0} | all-to-all | bytes 3145728 | tf_op jit(solution)/shard_map/all_to_all | solution.py:18
  236.3 0.2 convert_reduce_fusion.1
  236.6 1.0 fusion.20
  237.6 0.5 all-gather.14.cloned.1.call-start
  238.1 0.6 dynamic-slice
  238.7 5.2 %fusion.2 = f32[4,256,4,256]{3,1,2,0:T(8,128)} fusion(bf16[4,768,256]{2,1,0:T(8,128)(2,1)} %all-gather.10.cloned.1.call-done, bf16[4,768,256]{2,1,0:T(8,128)(2,1)S(1)} %copy-done.4), kind=kOutput, calls=%fused_computation.13 | convolution fusion | flops 1610612736 | bytes 7340032 | tf_op jit(solution)/shard_map/irh,jrd->jihd/dot_general | solution.py:55
  243.9 5.4 %copy.49 = f32[4,1,2,2,256,256]{5,4,2,1,0,3:T(8,128)} copy(f32[4,1,2,2,256,256]{4,5,3,2,0,1:T(8,128)} %bitcast.168) | data formatting | bytes 8388608 | tf_op jit(solution)/shard_map/stack | solution.py:57
  249.3 13.9 %all-gather.12.cloned.1.call-done = bf16[4,768,256]{2,1,0:T(8,128)(2,1)} async-done(((bf16[1,768,256]{2,1,0:T(8,128)(2,1)}), bf16[4,768,256]{2,1,0:T(8,128)(2,1)}) %all-gather.12.cloned.1.call-update) | async-done | bytes 1572880 | tf_op jit(solution)/shard_map/all_gather | solution.py:54
  263.2 5.2 %fusion.4 = f32[4,256,4,256]{3,1,2,0:T(8,128)} fusion(bf16[4,768,256]{2,1,0:T(8,128)(2,1)} %all-gather.12.cloned.1.call-done, bf16[4,768,256]{2,1,0:T(8,128)(2,1)S(1)} %copy-done.3), kind=kOutput, calls=%fused_computation.15 | convolution fusion | flops 1610612736 | bytes 7340032 | tf_op jit(solution)/shard_map/jrd,irh->jidh/dot_general | solution.py:56
  268.4 5.3 %copy.48 = f32[4,1,2,2,256,256]{5,4,2,1,0,3:T(8,128)} copy(f32[4,1,2,2,256,256]{4,5,0,3,2,1:T(8,128)} %bitcast.169) | data formatting | bytes 8388608 | tf_op jit(solution)/shard_map/stack | solution.py:57
  273.6 7.6 %maximum_bitcast_fusion = f32[2,4,2,2,256,256]{5,4,3,2,1,0:T(8,128)} fusion(f32[4,1,2,2,256,256]{5,4,2,1,0,3:T(8,128)} %copy.49, f32[4,1,2,2,256,256]{5,4,2,1,0,3:T(8,128)} %copy.48), kind=kLoop, calls=%fused_computation | loop fusion | flops 2097152 | bytes 16777216 | tf_op jit(solution)/shard_map/transpose | solution.py:58
  281.2 8.4 %reshape.194 = f32[2,4,262144]{2,1,0:T(4,128)} reshape(f32[2,4,2,2,256,256]{5,4,3,2,1,0:T(8,128)} %maximum_bitcast_fusion) | data formatting | bytes 16777216 | tf_op jit(solution)/shard_map/reshape | solution.py:59
  289.6 26.2 %all-reduce.2 = bf16[2,4,262144]{2,1,0:T(4,128)(2,1)} all-reduce(f32[2,4,262144]{2,1,0:T(4,128)} %reshape.194), channel_id=2, replica_groups=mesh['y'=4,'x'=4,'z'=4,'c'=2] {'c'}, use_global_device_ids=true, to_apply=%region_6.7.clone | all-reduce | flops 2097152 | bytes 12582912
  315.7 2.6 fusion
  318.4 0.5 broadcast.101
  318.9 4.6 %reduce.3 = bf16[4,262144]{1,0:T(4,128)(2,1)} reduce(bf16[4,1,262144]{2,0,1:T(4,128)(2,1)S(1)} %fusion, bf16[]{:T(256)} %broadcast.101), dimensions={1}, to_apply=%copy.50.reduce_sub_computation | reduce | bytes 4194306 | tf_op jit(solution)/shard_map/convert_element_type | solution.py:22
  323.5 5.0 %reshape.207 = bf16[4,2,131072]{2,1,0:T(2,128)(2,1)} reshape(bf16[4,262144]{1,0:T(4,128)(2,1)} %reduce.3) | data formatting | bytes 4194304
  328.5 30.3 %all_to_all.41 = bf16[4,2,131072]{2,1,0:T(2,128)(2,1)S(1)} all-to-all(bf16[4,2,131072]{2,1,0:T(2,128)(2,1)} %reshape.207), channel_id=1, replica_groups=mesh['y'=4,'x'=4,'z'=4,'c'=2] {'z'}, dimensions={0} | all-to-all | bytes 4194304 | tf_op jit(solution)/shard_map/all_to_all | solution.py:18
  358.8 3.4 reshape.208
  362.2 11.9 %convert_reduce_fusion = bf16[262144]{0:T(1024)(128)(2,1)S(1)} fusion(bf16[4,1,262144]{2,1,0:T(2,128)(2,1)} %reshape.208), kind=kLoop, calls=%fused_computation.2 | loop fusion | flops 1835008 | bytes 2621440 | tf_op jit(solution)/shard_map/reduce_sum | solution.py:23
  374.1 1.0 all_gather_reshape.4
  375.1 10.9 %all-gather.14.cloned.1.call-done = bf16[2,2,2,256,256]{4,3,2,1,0:T(8,128)(2,1)} async-done(((bf16[1,2,2,256,256]{4,3,2,1,0:T(8,128)(2,1)}), bf16[2,2,2,256,256]{4,3,2,1,0:T(8,128)(2,1)}) %all-gather.14.cloned.1.call-update) | async-done | bytes 1048592 | tf_op jit(solution)/shard_map/all_gather | solution.py:61
  386.0 1.3 copy.51
  387.3 0.5 convert_element_type.130
  387.8 7.4 %reduce.4 = bf16[4,131072]{1,0:T(4,128)(2,1)S(1)} reduce(bf16[4,1,131072]{2,1,0:T(2,128)(2,1)S(1)} %convert_element_type.130, bf16[]{:T(256)} %broadcast.101), dimensions={1}, to_apply=%convert_element_type.130.reduce_sub_computation | reduce | bytes 2097154 | tf_op jit(solution)/shard_map/convert_element_type | solution.py:63
  395.2 2.0 reshape.209
  397.3 4.3 all-to-all-start.6
  401.6 14.7 %all-to-all-done.6 = bf16[4,2,65536]{2,1,0:T(2,128)(2,1)S(1)} async-done(((bf16[4,2,65536]{2,1,0:T(2,128)(2,1)}), bf16[4,2,65536]{2,1,0:T(2,128)(2,1)S(1)}, u32[]{:S(2)}, u32[]{:S(2)}) %all-to-all-start.6) | async-done | bytes 1048608 | tf_op jit(solution)/shard_map/all_to_all | solution.py:18
  416.2 0.9 reshape.210
  417.2 6.4 %convert_reduce_fusion.4 = f32[4,131072]{1,0:T(4,128)S(1)} fusion(bf16[4,1,131072]{2,1,0:T(2,128)(2,1)S(1)} %reshape.210), kind=kLoop, calls=%fused_computation.11 | loop fusion | flops 524288 | bytes 3145728 | tf_op jit(solution)/shard_map/convert_element_type | solution.py:63
  423.6 0.4 copy.64
  424.0 0.1 dynamic-slice_bitcast_fusion
  424.1 0.9 slice_bitcast_fusion
  425.0 0.2 copy.53
  425.2 1.0 copy.54
  (19 shorter events, 0.1 us)
Async XLA Ops:
  7.2 2.5 copy-start.1
  7.2 32.7 %all-gather.6.cloned.1.call-start = ((), (), s32[]{:S(2)}) async-start(), calls=%async_computation.7 | async-start | bytes 1966080 | tf_op jit(solution)/shard_map/all_gather | solution.py:37
  9.6 106.0 %all-gather.8.cloned.1.call-start = ((), (), s32[]{:S(2)}) async-start(), calls=%async_computation.8 | async-start | bytes 1966080 | tf_op jit(solution)/shard_map/all_gather | solution.py:40
  66.4 1.7 copy-start.2
  120.7 24.3 %all-to-all-start.3 = ((bf16[4,768,256]{2,1,0:T(8,128)(2,1)}), bf16[4,768,256]{2,1,0:T(8,128)(2,1)}, u32[]{:S(2)}, u32[]{:S(2)}) async-start(bf16[4,768,256]{2,1,0:T(8,128)(2,1)} %fusion.16), calls=%async_computation.3 | async-start | bytes 3145728 | tf_op jit(solution)/shard_map/all_to_all | solution.py:18
  125.1 83.9 %all-gather.10.cloned.1.call-start = ((), (), s32[]{:S(2)}) async-start(), calls=%async_computation.9 | async-start | bytes 1966080 | tf_op jit(solution)/shard_map/all_gather | solution.py:50
  125.8 21.1 %copy-start = (f32[3,256,256]{2,1,0:T(8,128)S(1)}, f32[3,256,256]{2,1,0:T(8,128)}, u32[]{:S(2)}) copy-start(f32[3,256,256]{2,1,0:T(8,128)} %param.6) | copy-start | bytes 2359300
  177.1 86.1 %all-gather.12.cloned.1.call-start = ((), (), s32[]{:S(2)}) async-start(), calls=%async_computation.10 | async-start | bytes 1966080 | tf_op jit(solution)/shard_map/all_gather | solution.py:54
  236.3 1.8 copy-start.5
  236.3 2.4 copy-start.4
  237.6 148.4 %all-gather.14.cloned.1.call-start = ((), (), s32[]{:S(2)}) async-start(), calls=%async_computation.11 | async-start | bytes 1572864 | tf_op jit(solution)/shard_map/all_gather | solution.py:61
  243.9 19.3 %copy-start.3 = (bf16[4,768,256]{2,1,0:T(8,128)(2,1)S(1)}, bf16[4,768,256]{2,1,0:T(8,128)(2,1)}, u32[]{:S(2)}) copy-start(bf16[4,768,256]{2,1,0:T(8,128)(2,1)} %all-gather.6.cloned.1.call-done) | copy-start | bytes 4718596
  397.3 19.0 %all-to-all-start.6 = ((bf16[4,2,65536]{2,1,0:T(2,128)(2,1)}), bf16[4,2,65536]{2,1,0:T(2,128)(2,1)S(1)}, u32[]{:S(2)}, u32[]{:S(2)}) async-start(bf16[4,2,65536]{2,1,0:T(2,128)(2,1)} %reshape.209), calls=%async_computation.6 | async-start | bytes 2097152 | tf_op jit(solution)/shard_map/all_to_all | solution.py:18
Sparse Core Ops, SparseCore 0:
  10.2 29.4 all-gather.5
  67.8 47.8 all-gather.7
  177.2 31.6 all-gather.9
  237.7 25.4 all-gather.11
  375.2 10.7 all-gather.13
where the time goes:
time: 439 us; the launch traced here: 433 us
  blocking collectives  203 us (46%)
  waiting for transfers between devices  92.2 us (21%)
  other arithmetic  46.3 us (11%)
  local copies, waits for them, and re-layouts  45.3 us (10%)
  matrix products  22.5 us (5%)
  between operations  14.9 us (3%)
  starting transfers between devices  9.29 us (2%)
    all_to_all x5, blocking collectives, a2a(): return lax.all_to_all(array, axis, split_axis=0, concat_axis=0, tiled=True)  148 us
    all_to_all x2, waiting for transfers between devices, a2a(): return lax.all_to_all(array, axis, split_axis=0, concat_axis=0, tiled=True)  33.9 us
    all_gather x1, waiting for transfers between devices, on_device(): gg = lax.all_gather(gz, 'y')  31.8 us
    psum x1, blocking collectives, on_device(): both = lax.psum(jnp.stack([terms, norm]), DIM)  28.5 us
    unnamed x1, blocking collectives  26.2 us
    unnamed x20, local copies, waits for them, and re-layouts  16.3 us
    reduce_sum x4, other arithmetic, scatter_sum(): return jnp.sum(got.astype(jnp.float32), 0)  14.1 us
    all_gather x1, waiting for transfers between devices, on_device(): hg = lax.all_gather(gh, 'x')  13.9 us
  transfers between devices with their start and end apart: 7, of which 6 were waited for; matrix products, arithmetic and copies ran while one was open for 4% of the time, Pallas kernels for 0%

commit v1 on v0

--- a/solution.py
+++ b/solution.py
@@ -43,7 +43,7 @@
         (0.5 * lam_coef * time_step * z * z + z * inc).reshape(STEPS, rows, width), (0, 2)
     )
     norm = jnp.sum(states[STEPS] * states[STEPS], 1)
-    both = lax.psum(jnp.stack([terms, norm]), DIM)
+    both = lax.psum(lax.psum(jnp.stack([terms, norm]), axis_name="y"), axis_name="x")
     residual = initial + both[0] - jnp.log((1.0 + both[1]) * 0.5)
     scale = jnp.tile(zscale * residual, STEPS)[:, None]
     gz = (scale * (lam_coef * time_step * z + inc)).astype(bf16)

time: 439 us -> 421 us (0.959)
  blocking collectives: 203 us -> 187 us
    psum x1 -> x2, blocking collectives: 28.5 us -> 12.9 us  [the longest x1 6.88 us: on_device(): lax.psum(jnp.stack([terms, norm]), axis_name='y')]
where the time goes in v1:
time: 421 us; the launch traced here: 414 us
  blocking collectives  187 us (44%)
  waiting for transfers between devices  89.3 us (21%)
  other arithmetic  46.3 us (11%)
  local copies, waits for them, and re-layouts  45.3 us (11%)
  matrix products  22.5 us (5%)
  between operations  14.9 us (4%)
  starting transfers between devices  9.29 us (2%)
    all_to_all x5, blocking collectives, a2a(): return lax.all_to_all(array, axis, split_axis=0, concat_axis=0, tiled=True)  148 us
    all_to_all x2, waiting for transfers between devices, a2a(): return lax.all_to_all(array, axis, split_axis=0, concat_axis=0, tiled=True)  33.9 us
    all_gather x1, waiting for transfers between devices, on_device(): gg = lax.all_gather(gz, 'y')  28.9 us
    unnamed x1, blocking collectives  26.2 us
    unnamed x20, local copies, waits for them, and re-layouts  16.3 us
    reduce_sum x4, other arithmetic, scatter_sum(): return jnp.sum(got.astype(jnp.float32), 0)  14.1 us
    all_gather x1, waiting for transfers between devices, on_device(): hg = lax.all_gather(gh, 'x')  13.9 us
    all_gather x1, waiting for transfers between devices, on_device(): grads = lax.all_gather(grads, 'c')  10.9 us
  transfers between devices with their start and end apart: 7, of which 6 were waited for; matrix products, arithmetic and copies ran while one was open for 4% of the time, Pallas kernels for 0%

profile of v1, /device:TPU:1, one launch (start us, length us, event | category | flops | bytes accessed | tf_op | source)
XLA Modules:
  0.0 414.4 jit_solution(2776035961903867730)
XLA Ops:
  7.2 0.0 all-gather.6.cloned.1.call-start
  7.2 1.6 convert_bitcast_fusion.2
  8.8 0.8 pad_maximum_fusion
  9.6 0.0 all-gather.8.cloned.1.call-start
  9.7 0.1 copy.66
  9.8 30.1 %all_to_all.37 = bf16[4,4,256,256]{3,2,1,0:T(8,128)(2,1)S(1)} all-to-all(bf16[4,4,256,256]{3,2,1,0:T(8,128)(2,1)S(1)} %bitcast.164), channel_id=1, replica_groups=mesh['y'=4,'x'=4,'z'=4,'c'=2] {'x'}, dimensions={0} | all-to-all | bytes 4194304 | tf_op jit(solution)/shard_map/all_to_all | solution.py:18
  39.9 3.2 fusion.10
  43.1 23.3 %all_to_all.38 = bf16[4,768,256]{2,1,0:T(8,128)(2,1)S(1)} all-to-all(bf16[4,768,256]{2,1,0:T(8,128)(2,1)S(1)} %fusion.10), channel_id=1, replica_groups=mesh['y'=4,'x'=4,'z'=4,'c'=2] {'x'}, dimensions={0} | all-to-all | bytes 3145728 | tf_op jit(solution)/shard_map/all_to_all | solution.py:18
  66.4 0.2 convert_reduce_fusion.3
  66.7 1.0 fusion.26
  67.7 0.5 copy-done.2
  68.2 2.5 copy.43
  70.6 2.8 copy.44
  73.4 40.7 %all_to_all.39 = bf16[4,4,256,256]{3,2,1,0:T(8,128)(2,1)} all-to-all(bf16[4,4,256,256]{3,2,1,0:T(8,128)(2,1)S(1)} %copy.44), channel_id=1, replica_groups=mesh['y'=4,'x'=4,'z'=4,'c'=2] {'x'}, dimensions={0} | all-to-all | bytes 4194304 | tf_op jit(solution)/shard_map/all_to_all | solution.py:18
  114.1 1.5 all-gather.8.cloned.1.call-done
  115.6 5.1 %fusion.16 = bf16[4,768,256]{2,1,0:T(8,128)(2,1)} fusion(bf16[4,4,256,256]{3,2,1,0:T(8,128)(2,1)} %all_to_all.39, bf16[4,768,256]{2,1,0:T(8,128)(2,1)} %all-gather.8.cloned.1.call-done), kind=kOutput, calls=%fused_computation.23 | convolution fusion | flops 1611399168 | bytes 5242880 | tf_op jit(solution)/shard_map/irh,ijhd->jrd/dot_general | solution.py:41
  120.7 4.3 %all-to-all-start.3 = ((bf16[4,768,256]{2,1,0:T(8,128)(2,1)}), bf16[4,768,256]{2,1,0:T(8,128)(2,1)}, u32[]{:S(2)}, u32[]{:S(2)}) async-start(bf16[4,768,256]{2,1,0:T(8,128)(2,1)} %fusion.16), calls=%async_computation.3 | async-start | bytes 3145728 | tf_op jit(solution)/shard_map/all_to_all | solution.py:18
  125.1 0.0 all-gather.10.cloned.1.call-start
  125.8 19.2 %all-to-all-done.3 = bf16[4,768,256]{2,1,0:T(8,128)(2,1)} async-done(((bf16[4,768,256]{2,1,0:T(8,128)(2,1)}), bf16[4,768,256]{2,1,0:T(8,128)(2,1)}, u32[]{:S(2)}, u32[]{:S(2)}) %all-to-all-start.3) | async-done | bytes 1572896 | tf_op jit(solution)/shard_map/all_to_all | solution.py:18
  145.0 1.7 convert_reduce_fusion.2
  146.7 0.1 broadcast_multiply_fusion.1
  146.9 0.2 multiply_reduce_fusion
  147.1 6.9 %psum.14 = f32[2,256]{1,0:T(2,128)S(1)} all-reduce(f32[2,256]{1,0:T(2,128)S(1)} %pad_maximum_fusion.1), channel_id=1, replica_groups=mesh['y'=4,'x'=4,'z'=4,'c'=2] {'y'}, use_global_device_ids=true, to_apply=%region_4.5 | all-reduce | flops 512 | bytes 4096 | tf_op jit(solution)/shard_map/psum | solution.py:46
  153.9 6.0 %psum.15 = f32[2,256]{1,0:T(2,128)S(1)} all-reduce(f32[2,256]{1,0:T(2,128)S(1)} %psum.14), channel_id=1, replica_groups=mesh['y'=4,'x'=4,'z'=4,'c'=2] {'x'}, use_global_device_ids=true, to_apply=%region_5.6 | all-reduce | flops 512 | bytes 4096 | tf_op jit(solution)/shard_map/psum | solution.py:46
  159.9 0.6 broadcast_multiply_fusion.2
  160.5 0.9 fusion.22
  161.5 0.0 all-gather.12.cloned.1.call-start
  161.5 28.9 %all-gather.10.cloned.1.call-done = bf16[4,768,256]{2,1,0:T(8,128)(2,1)} async-done(((bf16[1,768,256]{2,1,0:T(8,128)(2,1)}), bf16[4,768,256]{2,1,0:T(8,128)(2,1)}) %all-gather.10.cloned.1.call-update) | async-done | bytes 1572880 | tf_op jit(solution)/shard_map/all_gather | solution.py:50
  190.4 3.9 fusion.13
  194.3 23.5 %all_to_all.40 = bf16[4,768,256]{2,1,0:T(8,128)(2,1)S(1)} all-to-all(bf16[4,768,256]{2,1,0:T(8,128)(2,1)S(1)} %fusion.13), channel_id=1, replica_groups=mesh['y'=4,'x'=4,'z'=4,'c'=2] {'x'}, dimensions={0} | all-to-all | bytes 3145728 | tf_op jit(solution)/shard_map/all_to_all | solution.py:18
  217.8 0.2 convert_reduce_fusion.1
  218.0 1.0 fusion.20
  219.1 0.5 all-gather.14.cloned.1.call-start
  219.6 0.6 dynamic-slice
  220.2 5.2 %fusion.2 = f32[4,256,4,256]{3,1,2,0:T(8,128)} fusion(bf16[4,768,256]{2,1,0:T(8,128)(2,1)} %all-gather.10.cloned.1.call-done, bf16[4,768,256]{2,1,0:T(8,128)(2,1)S(1)} %copy-done.4), kind=kOutput, calls=%fused_computation.13 | convolution fusion | flops 1610612736 | bytes 7340032 | tf_op jit(solution)/shard_map/irh,jrd->jihd/dot_general | solution.py:55
  225.4 5.4 %copy.49 = f32[4,1,2,2,256,256]{5,4,2,1,0,3:T(8,128)} copy(f32[4,1,2,2,256,256]{4,5,3,2,0,1:T(8,128)} %bitcast.168) | data formatting | bytes 8388608 | tf_op jit(solution)/shard_map/stack | solution.py:57
  230.8 13.9 %all-gather.12.cloned.1.call-done = bf16[4,768,256]{2,1,0:T(8,128)(2,1)} async-done(((bf16[1,768,256]{2,1,0:T(8,128)(2,1)}), bf16[4,768,256]{2,1,0:T(8,128)(2,1)}) %all-gather.12.cloned.1.call-update) | async-done | bytes 1572880 | tf_op jit(solution)/shard_map/all_gather | solution.py:54
  244.7 5.2 %fusion.4 = f32[4,256,4,256]{3,1,2,0:T(8,128)} fusion(bf16[4,768,256]{2,1,0:T(8,128)(2,1)} %all-gather.12.cloned.1.call-done, bf16[4,768,256]{2,1,0:T(8,128)(2,1)S(1)} %copy-done.3), kind=kOutput, calls=%fused_computation.15 | convolution fusion | flops 1610612736 | bytes 7340032 | tf_op jit(solution)/shard_map/jrd,irh->jidh/dot_general | solution.py:56
  249.8 5.3 %copy.48 = f32[4,1,2,2,256,256]{5,4,2,1,0,3:T(8,128)} copy(f32[4,1,2,2,256,256]{4,5,0,3,2,1:T(8,128)} %bitcast.169) | data formatting | bytes 8388608 | tf_op jit(solution)/shard_map/stack | solution.py:57
  255.1 7.6 %maximum_bitcast_fusion = f32[2,4,2,2,256,256]{5,4,3,2,1,0:T(8,128)} fusion(f32[4,1,2,2,256,256]{5,4,2,1,0,3:T(8,128)} %copy.49, f32[4,1,2,2,256,256]{5,4,2,1,0,3:T(8,128)} %copy.48), kind=kLoop, calls=%fused_computation | loop fusion | flops 2097152 | bytes 16777216 | tf_op jit(solution)/shard_map/transpose | solution.py:58
  262.7 8.4 %reshape.194 = f32[2,4,262144]{2,1,0:T(4,128)} reshape(f32[2,4,2,2,256,256]{5,4,3,2,1,0:T(8,128)} %maximum_bitcast_fusion) | data formatting | bytes 16777216 | tf_op jit(solution)/shard_map/reshape | solution.py:59
  271.0 26.2 %all-reduce.2 = bf16[2,4,262144]{2,1,0:T(4,128)(2,1)} all-reduce(f32[2,4,262144]{2,1,0:T(4,128)} %reshape.194), channel_id=2, replica_groups=mesh['y'=4,'x'=4,'z'=4,'c'=2] {'c'}, use_global_device_ids=true, to_apply=%region_7.8.clone | all-reduce | flops 2097152 | bytes 12582912
  297.2 2.6 fusion
  299.8 0.5 broadcast.101
  300.4 4.6 %reduce.3 = bf16[4,262144]{1,0:T(4,128)(2,1)} reduce(bf16[4,1,262144]{2,0,1:T(4,128)(2,1)S(1)} %fusion, bf16[]{:T(256)} %broadcast.101), dimensions={1}, to_apply=%copy.50.reduce_sub_computation | reduce | bytes 4194306 | tf_op jit(solution)/shard_map/convert_element_type | solution.py:22
  305.0 5.0 %reshape.207 = bf16[4,2,131072]{2,1,0:T(2,128)(2,1)} reshape(bf16[4,262144]{1,0:T(4,128)(2,1)} %reduce.3) | data formatting | bytes 4194304
  310.0 30.3 %all_to_all.41 = bf16[4,2,131072]{2,1,0:T(2,128)(2,1)S(1)} all-to-all(bf16[4,2,131072]{2,1,0:T(2,128)(2,1)} %reshape.207), channel_id=1, replica_groups=mesh['y'=4,'x'=4,'z'=4,'c'=2] {'z'}, dimensions={0} | all-to-all | bytes 4194304 | tf_op jit(solution)/shard_map/all_to_all | solution.py:18
  340.3 3.4 reshape.208
  343.6 11.9 %convert_reduce_fusion = bf16[262144]{0:T(1024)(128)(2,1)S(1)} fusion(bf16[4,1,262144]{2,1,0:T(2,128)(2,1)} %reshape.208), kind=kLoop, calls=%fused_computation.2 | loop fusion | flops 1835008 | bytes 2621440 | tf_op jit(solution)/shard_map/reduce_sum | solution.py:23
  355.6 1.0 all_gather_reshape.4
  356.6 10.9 %all-gather.14.cloned.1.call-done = bf16[2,2,2,256,256]{4,3,2,1,0:T(8,128)(2,1)} async-done(((bf16[1,2,2,256,256]{4,3,2,1,0:T(8,128)(2,1)}), bf16[2,2,2,256,256]{4,3,2,1,0:T(8,128)(2,1)}) %all-gather.14.cloned.1.call-update) | async-done | bytes 1048592 | tf_op jit(solution)/shard_map/all_gather | solution.py:61
  367.5 1.3 copy.51
  368.8 0.5 convert_element_type.130
  369.3 7.4 %reduce.4 = bf16[4,131072]{1,0:T(4,128)(2,1)S(1)} reduce(bf16[4,1,131072]{2,1,0:T(2,128)(2,1)S(1)} %convert_element_type.130, bf16[]{:T(256)} %broadcast.101), dimensions={1}, to_apply=%convert_element_type.130.reduce_sub_computation | reduce | bytes 2097154 | tf_op jit(solution)/shard_map/convert_element_type | solution.py:63
  376.7 2.0 reshape.209
  378.7 4.3 %all-to-all-start.6 = ((bf16[4,2,65536]{2,1,0:T(2,128)(2,1)}), bf16[4,2,65536]{2,1,0:T(2,128)(2,1)S(1)}, u32[]{:S(2)}, u32[]{:S(2)}) async-start(bf16[4,2,65536]{2,1,0:T(2,128)(2,1)} %reshape.209), calls=%async_computation.6 | async-start | bytes 2097152 | tf_op jit(solution)/shard_map/all_to_all | solution.py:18
  383.0 14.7 %all-to-all-done.6 = bf16[4,2,65536]{2,1,0:T(2,128)(2,1)S(1)} async-done(((bf16[4,2,65536]{2,1,0:T(2,128)(2,1)}), bf16[4,2,65536]{2,1,0:T(2,128)(2,1)S(1)}, u32[]{:S(2)}, u32[]{:S(2)}) %all-to-all-start.6) | async-done | bytes 1048608 | tf_op jit(solution)/shard_map/all_to_all | solution.py:18
  397.7 0.9 reshape.210
  398.7 6.4 %convert_reduce_fusion.4 = f32[4,131072]{1,0:T(4,128)S(1)} fusion(bf16[4,1,131072]{2,1,0:T(2,128)(2,1)S(1)} %reshape.210), kind=kLoop, calls=%fused_computation.11 | loop fusion | flops 524288 | bytes 3145728 | tf_op jit(solution)/shard_map/convert_element_type | solution.py:63
  405.1 0.4 copy.64
  405.5 0.1 dynamic-slice_bitcast_fusion
  405.6 0.9 slice_bitcast_fusion
  406.5 0.2 copy.53
  406.7 1.0 copy.54
  (20 shorter events, 0.1 us)
Async XLA Ops:
  7.2 2.5 copy-start.1
  7.2 32.7 %all-gather.6.cloned.1.call-start = ((), (), s32[]{:S(2)}) async-start(), calls=%async_computation.7 | async-start | bytes 1966080 | tf_op jit(solution)/shard_map/all_gather | solution.py:37
  9.6 106.0 %all-gather.8.cloned.1.call-start = ((), (), s32[]{:S(2)}) async-start(), calls=%async_computation.8 | async-start | bytes 1966080 | tf_op jit(solution)/shard_map/all_gather | solution.py:40
  66.4 1.7 copy-start.2
  120.7 24.3 %all-to-all-start.3 = ((bf16[4,768,256]{2,1,0:T(8,128)(2,1)}), bf16[4,768,256]{2,1,0:T(8,128)(2,1)}, u32[]{:S(2)}, u32[]{:S(2)}) async-start(bf16[4,768,256]{2,1,0:T(8,128)(2,1)} %fusion.16), calls=%async_computation.3 | async-start | bytes 3145728 | tf_op jit(solution)/shard_map/all_to_all | solution.py:18
  125.1 65.3 %all-gather.10.cloned.1.call-start = ((), (), s32[]{:S(2)}) async-start(), calls=%async_computation.9 | async-start | bytes 1966080 | tf_op jit(solution)/shard_map/all_gather | solution.py:50
  125.8 21.1 %copy-start = (f32[3,256,256]{2,1,0:T(8,128)S(1)}, f32[3,256,256]{2,1,0:T(8,128)}, u32[]{:S(2)}) copy-start(f32[3,256,256]{2,1,0:T(8,128)} %param.6) | copy-start | bytes 2359300
  161.5 83.2 %all-gather.12.cloned.1.call-start = ((), (), s32[]{:S(2)}) async-start(), calls=%async_computation.10 | async-start | bytes 1966080 | tf_op jit(solution)/shard_map/all_gather | solution.py:54
  217.8 1.8 copy-start.5
  217.8 2.4 copy-start.4
  219.1 148.4 %all-gather.14.cloned.1.call-start = ((), (), s32[]{:S(2)}) async-start(), calls=%async_computation.11 | async-start | bytes 1572864 | tf_op jit(solution)/shard_map/all_gather | solution.py:61
  225.3 19.3 %copy-start.3 = (bf16[4,768,256]{2,1,0:T(8,128)(2,1)S(1)}, bf16[4,768,256]{2,1,0:T(8,128)(2,1)}, u32[]{:S(2)}) copy-start(bf16[4,768,256]{2,1,0:T(8,128)(2,1)} %all-gather.6.cloned.1.call-done) | copy-start | bytes 4718596
  378.7 19.0 %all-to-all-start.6 = ((bf16[4,2,65536]{2,1,0:T(2,128)(2,1)}), bf16[4,2,65536]{2,1,0:T(2,128)(2,1)S(1)}, u32[]{:S(2)}, u32[]{:S(2)}) async-start(bf16[4,2,65536]{2,1,0:T(2,128)(2,1)} %reshape.209), calls=%async_computation.6 | async-start | bytes 2097152 | tf_op jit(solution)/shard_map/all_to_all | solution.py:18
Sparse Core Ops, SparseCore 0:
  10.2 29.4 all-gather.5
  67.8 47.8 all-gather.7
  161.6 28.7 all-gather.9
  219.2 25.4 all-gather.11
  356.7 10.7 all-gather.13
